TPU v7x, 32 devices: a whole 2x2x4 slice. The times are simulated.
32 devices in a mesh: groups: 2 (over x), tp: 8 (over z, y), role: 2 (over core).
Axes of the slice: x: 2, y: 2, z: 4, core: 2. Of those that a mesh axis runs over, the one named last changes fastest.
Arguments:
- rows_in: bfloat16 [2, 1024, 8192], P('role', 'groups', 'tp'), parts along dimension 1, may hold values from -6 to 6
- norm_gain: bfloat16 [8192], replicated, may hold values from 0.5 to 4
- q_words: int32 [1024, 8192], P(None, 'tp'), may hold values from -2147483648 to 2147483646
- q_scales: bfloat16 [64, 8192], P(None, 'tp'), may hold values from 0.0011978149 to 0.0047912598
- kv_words: int32 [8, 1024, 256], P('tp'), may hold values from -2147483648 to 2147483646, as said below
- kv_scales: bfloat16 [8, 64, 256], P('tp'), may hold values from 0.0012 to 0.0048, as said below
- o_words: int32 [1024, 8192], P('tp'), may hold values from -2147483648 to 2147483646
- o_scales: bfloat16 [64, 8192], P('tp'), may hold values from 0.0011978149 to 0.0047912598
- kv_pool: bfloat16 [8, 2048, 16, 256], P('tp', 'groups'), parts along dimension 1, may hold values from -120 to 120, as said below
- prompt_pages: int32 [32], P('groups'), parts along dimension 0, may hold values from 1 to 8, 32 in all
- page_slots: int32 [64], P('groups'), parts along dimension 0, may hold values from 0 to 1023, as said below
- block_tables: int32 [992, 16], P('groups'), parts along dimension 0, may hold values from 0 to 1023, as said below
- cache_lens: int32 [992], P('groups'), parts along dimension 0, may hold values from 1 to 256
Outputs:
- layer_out: bfloat16 [2, 1024, 8192], P('role', 'groups', 'tp'), parts along dimension 1
There are 2 independent parts, one for each index of `groups`. A program takes and returns all parts, laid end to end along the dimension named above; an argument that names none is the same for every part. Nothing has to cross between parts.
Inputs may be any that keep to these rules, and one draw needn't show every extreme that they name: `kv_words`: entries t and u are equal whenever t * 8 // 8 equals u * 8 // 8. `kv_scales`: entries t and u are equal whenever t * 8 // 8 equals u * 8 // 8. `kv_pool`: entries t and u are equal whenever t * 8 // 8 equals u * 8 // 8. `page_slots`: distinct pages; entry j receives the j-th page of the prompts taken in order. `block_tables`: no entry is one of page_slots; sequences may share pages.
All inputs are finite; a program needn't handle non-finite values.
Results may differ from a plain program's by a relative error of at most 0.015.
The roundings to bfloat16 on the way count: a program that leaves them out, or rounds other values in their place, can miss the bound.
Values may be sent and summed in bfloat16 or wider, within the bound.
A program may use at most 192 MiB of HBM per device.

v0:
```python
import jax
import jax.numpy as jnp
from jax import lax
from jax.sharding import PartitionSpec as P

HD = 128


def passed_along(block, axis, distance):
    devices = range(lax.axis_size(axis))
    route = [(i - distance, i) for i in devices if i - distance in devices]
    return lax.ppermute(block, axis, route)


def unpack_words(words, scales):
    shifts = jnp.arange(8, dtype=jnp.int32) * 4
    nibbles = jnp.bitwise_and(jnp.right_shift(words[:, None, :], shifts[None, :, None]), 15) - 8
    values = nibbles.reshape(words.shape[0] * 8, words.shape[1]).astype(jnp.float32)
    group = values.shape[0] // scales.shape[0]
    spread = jnp.repeat(scales.astype(jnp.float32), group, axis=0)
    return (values * spread).astype(jnp.bfloat16)


def rms_normed(rows, gain):
    wide = rows.astype(jnp.float32)
    inverse = lax.rsqrt(jnp.mean(wide * wide, axis=-1, keepdims=True) + 1e-05)
    return (wide * inverse * gain.astype(jnp.float32)).astype(jnp.bfloat16)


def rotate(heads, positions):
    half = heads.shape[-1] // 2
    freq = 500000.0 ** (-jnp.arange(half, dtype=jnp.float32) * 2.0 / heads.shape[-1])
    angle = positions.astype(jnp.float32)[:, None, None] * freq[None, None, :]
    cosine = jnp.cos(angle)
    sine = jnp.sin(angle)
    first = heads[..., :half]
    second = heads[..., half:]
    return jnp.concatenate(
        [first * cosine - second * sine, second * cosine + first * sine], axis=-1
    )


def layout(prompt_pages, page_slots, block_tables, cache_lens, rows):
    page = rows // page_slots.shape[0]
    count = prompt_pages.shape[0]
    ends = jnp.cumsum(prompt_pages) * page
    starts = ends - prompt_pages * page
    index = jnp.arange(rows, dtype=jnp.int32)
    member = (index[:, None] >= starts[None, :]) & (index[:, None] < ends[None, :])
    doc = jnp.sum(jnp.where(member, jnp.arange(count, dtype=jnp.int32)[None, :], 0), axis=1)
    prefill_pos = index - jnp.sum(jnp.where(member, starts[None, :], 0), axis=1)
    span = block_tables.shape[1]
    picks = jnp.minimum(
        starts[:, None] // page + jnp.arange(span, dtype=jnp.int32)[None, :],
        page_slots.shape[0] - 1,
    )
    prompt_table = page_slots[picks]
    table = jnp.concatenate([prompt_table, block_tables], axis=0)
    lengths = jnp.concatenate([prompt_pages * page, cache_lens])
    return (doc, prefill_pos, table, lengths)


def prefill_attend(query, keys, values, doc):
    rows = query.shape[0]
    block = min(512, rows)
    score_scale = query.shape[-1] ** (-0.5)
    index = jnp.arange(rows, dtype=jnp.int32)

    def prefill_one_block(start):
        logit_scores = (
            jnp.einsum("qhd,kd->hqk", query, keys, preferred_element_type=jnp.float32) * score_scale
        )
        own = start + jnp.arange(block, dtype=jnp.int32)
        allowed = (doc[:, None] == doc[None, :]) & (index[None, :] <= own[:, None])
        logit_scores = jnp.where(allowed[None], logit_scores, -1e30)
        attention_probs = jax.nn.softmax(logit_scores, axis=-1).astype(jnp.bfloat16)
        return jnp.einsum(
            "hqk,kd->qhd", attention_probs, values, preferred_element_type=jnp.float32
        ).astype(jnp.bfloat16)

    starts = jnp.arange(0, rows, block, dtype=jnp.int32)
    done = lax.map(prefill_one_block, starts)
    return done.reshape(rows, query.shape[1], query.shape[2])


def decode_attend(query, key_self, value_self, cache, table, lengths):
    rows = query.shape[0]
    block = min(128, rows)
    score_scale = query.shape[-1] ** (-0.5)
    head_dim = query.shape[-1]

    def decode_one_block(start):
        partial_query = lax.dynamic_slice_in_dim(query, start, block, 0)
        part_table = lax.dynamic_slice_in_dim(table, start, block, 0)
        part_len = lax.dynamic_slice_in_dim(lengths, start, block, 0)
        pages = cache[part_table]
        pages = pages.reshape(block, pages.shape[1] * pages.shape[2], pages.shape[3])
        own_key = lax.dynamic_slice_in_dim(key_self, start, block, 0)
        own_value = lax.dynamic_slice_in_dim(value_self, start, block, 0)
        gathered_keys = jnp.concatenate([pages[..., :head_dim], own_key[:, None, :]], axis=1)
        gathered_values = jnp.concatenate([pages[..., head_dim:], own_value[:, None, :]], axis=1)
        logit_scores = (
            jnp.einsum(
                "jai,jri->jar", partial_query, gathered_keys, preferred_element_type=jnp.float32
            )
            * score_scale
        )
        spots = jnp.arange(pages.shape[1], dtype=jnp.int32)
        valid = jnp.concatenate(
            [spots[None, :] < part_len[:, None], jnp.ones((block, 1), dtype=bool)], axis=1
        )
        logit_scores = jnp.where(valid[:, None, :], logit_scores, -1e30)
        attention_probs = jax.nn.softmax(logit_scores, axis=-1).astype(jnp.bfloat16)
        return jnp.einsum(
            "cwt,ctr->cwr", attention_probs, gathered_values, preferred_element_type=jnp.float32
        ).astype(jnp.bfloat16)

    starts = jnp.arange(0, rows, block, dtype=jnp.int32)
    done = lax.map(decode_one_block, starts)
    return done.reshape(rows, query.shape[1], query.shape[2])


def local(
    rows_in,
    norm_gain,
    q_words,
    q_scales,
    kv_words,
    kv_scales,
    o_words,
    o_scales,
    kv_pool,
    prompt_pages,
    page_slots,
    block_tables,
    cache_lens,
):
    side = lax.axis_index("role")
    whole = lax.all_gather(rows_in[0], "tp", axis=1, tiled=True)
    rows = whole.shape[0]
    normed = rms_normed(whole, norm_gain)
    doc, prefill_pos, table, lengths = layout(
        prompt_pages, page_slots, block_tables, cache_lens, rows
    )
    positions = jnp.where(side == 0, prefill_pos, lengths)
    w_query = unpack_words(q_words, q_scales)
    w_keyval = unpack_words(kv_words[0], kv_scales[0])
    projected = jnp.dot(normed, w_query, preferred_element_type=jnp.float32)
    query = rotate(projected.reshape(rows, -1, HD), positions).astype(jnp.bfloat16)
    keyval = jnp.dot(normed, w_keyval, preferred_element_type=jnp.float32)
    key_new = rotate(keyval[:, None, :HD], positions)[:, 0].astype(jnp.bfloat16)
    value_new = keyval[:, HD:].astype(jnp.bfloat16)
    fresh = jnp.concatenate([key_new, value_new], axis=1)
    arrived = passed_along(fresh, "role", 1)
    pool = kv_pool[0]

    def run_prefill():
        return prefill_attend(query, key_new, value_new, doc)

    def run_decode():
        cache = pool.at[page_slots].set(arrived.reshape(-1, pool.shape[1], pool.shape[2]))
        return decode_attend(query, key_new, value_new, cache, table, lengths)

    attention_output = lax.cond(side == 0, run_prefill, run_decode).reshape(rows, -1)
    column_words, column_scales = (
        lax.all_to_all(o_words, "tp", split_axis=1, concat_axis=0, tiled=True),
        lax.all_to_all(o_scales, "tp", split_axis=1, concat_axis=0, tiled=True),
    )
    w_columns = unpack_words(column_words, column_scales)
    summed = jnp.dot(
        lax.all_gather(attention_output, "tp", axis=1, tiled=True),
        w_columns,
        preferred_element_type=jnp.float32,
    )
    return summed.astype(jnp.bfloat16)[None]


def solution(mesh):
    return jax.shard_map(
        local,
        mesh=mesh,
        in_specs=(
            P("role", "groups", "tp"),
            P(),
            P(None, "tp"),
            P(None, "tp"),
            P("tp", None, None),
            P("tp", None, None),
            P("tp", None),
            P("tp", None),
            P("tp", "groups", None, None),
            P("groups"),
            P("groups"),
            P("groups", None),
            P("groups"),
        ),
        out_specs=P("role", "groups", "tp"),
        check_vma=False,
    )
```

profile of v0, /device:TPU:0, one launch (start us, length us, event | category | flops | bytes accessed | tf_op | source)
XLA Modules:
  0.0 630.2 jit_solution(2411053265637678212)
XLA Ops:
  6.5 7.1 %copy.117 = bf16[1,1024,16,256]{3,2,1,0:T(8,128)(2,1)} copy(bf16[1,1024,16,256]{3,2,1,0:T(8,128)(2,1)} %param.25) | data formatting | bytes 16777216
  13.7 0.0 all-gather.6.cloned.1.call-update
  13.7 7.3 %all-to-all-start.1 = ((bf16[8,8,1024]{2,0,1:T(8,128)(2,1)}), bf16[8,8,1024]{2,0,1:T(8,128)(2,1)S(1)}, u32[]{:S(2)}, u32[]{:S(2)}) async-start(bf16[8,8,1024]{2,0,1:T(8,128)(2,1)} %bitcast.31), calls=%async_computation.1 | async-start | bytes 262144 | tf_op jit(solution)/shard_map/all_to_all | solution.py:167
  21.0 0.0 copy-start.3
  21.0 0.0 copy-start.6
  21.0 0.0 copy-start
  21.1 5.8 copy.76
  26.9 1.6 all-to-all-done.1
  28.5 4.7 all-to-all-start
  33.1 0.0 copy-start.5
  33.2 0.0 copy-start.8
  33.2 0.0 all-gather.4.cloned.1.call-start
  33.2 0.0 copy-done.7
  33.2 0.1 copy.64
  33.4 0.3 shift_right_arithmetic.68
  33.7 0.1 multiply_reduce_fusion
  33.8 0.1 compare_select_fusion.2
  33.9 0.1 reshape.345
  34.0 1.9 gather_fusion.1
  35.9 0.1 reshape.344
  36.0 0.1 copy.66
  36.1 3.3 fusion.56
  39.4 0.1 pad_add_fusion
  39.5 0.1 select_reduce_fusion.1
  39.6 0.1 select_convert_fusion
  39.7 0.1 fusion.72
  39.8 0.5 multiply_cosine_fusion
  40.3 168.6 %all-to-all-done = s32[128,8,1024]{0,2,1:T(8,128)} async-done(((s32[128,8,1024]{0,2,1:T(8,128)}), s32[128,8,1024]{0,2,1:T(8,128)}, u32[]{:S(2)}, u32[]{:S(2)}) %all-to-all-start) | async-done | bytes 4194336 | tf_op jit(solution)/shard_map/all_to_all | solution.py:166
  209.0 5.4 copy.77
  214.4 17.7 %fusion.43 = (bf16[8192,1024]{1,0:T(8,128)(2,1)}, bf16[8192,1024]{1,0:T(8,128)(2,1)}) fusion(f32[64,1024]{1,0:T(8,128)S(1)} %convert_bitcast_fusion, s32[1024,1024]{1,0:T(8,128)} %bitcast.137, s32[8192]{0:T(1024)S(1)} %shift_right_arithmetic.68, f32[64,1024]{1,0:T(8,128)S(1)} %convert_element_type.93, s32[1024,1024]{1,0:T(8,128)} %param.19), kind=kLoop, calls=%fused_computation.53 | loop fusion | flops 100663296 | bytes 42500096 | tf_op jit(solution)/shard_map/convert_element_type | solution.py:21
  232.1 21.3 %copy.84 = bf16[1024,8192]{1,0:T(8,128)(2,1)} copy(bf16[1024,8192]{0,1:T(8,128)(2,1)} %bitcast.136) | data formatting | bytes 33554432 | tf_op jit(solution)/shard_map/dot_general | solution.py:148
  253.3 5.3 fusion.51
  258.6 0.5 copy-done.1
  259.1 5.1 fusion.61
  264.2 0.6 fusion.69
  264.8 1.5 collective-permute-start
  266.3 12.3 %fusion.54 = f32[512,8,128]{0,2,1:T(8,128)S(1)} fusion(bf16[8,128,8192]{2,1,0:T(8,128)(2,1)} %bitcast.138, bf16[1,512,8192]{2,1,0:T(8,128)(2,1)S(1)} %copy-done.1, f32[8192]{0:T(1024)S(1)} %convert_element_type.84, f32[512]{0:T(512)S(1)} %add_rsqrt_fusion), kind=kOutput, calls=%fused_computation.69 | convolution fusion | flops 8606711808 | bytes 27297792 | tf_op jit(solution)/shard_map/dot_general | solution.py:148
  278.6 0.4 subtract_convert_fusion
  279.0 0.1 pad_maximum_fusion
  279.1 0.0 collective-permute-done
  279.1 10.4 %conditional.1 = (bf16[512,8,128]{2,0,1:T(8,128)(2,1)S(1)}) conditional(s32[]{:T(128)} %convert_element_type.82, (bf16[1,1024,16,256]{3,2,1,0:T(8,128)(2,1)}, s32[32]{0:T(128)S(1)}, bf16[512,256]{0,1:T(8,128)(2,1)S(1)}, s32[512]{0:T(512)S(1)}, bf16[512,8,128]{0,2,1:T(8,128)(2,1)S(1)}, /*index=5*/s32[512,16]{0,1:T(8,128)S(1)}, ...), branch_computations={%region_3.9_spmd, %region_9.13_spmd} | conditional | flops 1087651840 | bytes 90089912 | solution.py:164
  279.2 0.2 fusion.8
  279.4 5.2 fusion.75
  284.6 4.7 fusion.7
  289.5 1.3 copy.75
  290.8 0.0 all-gather.4.cloned.1.call-update
  290.8 316.9 %all-gather.4.cloned.1.call-done = bf16[512,8192]{0,1:T(8,128)(2,1)} async-done(((bf16[512,1024]{0,1:T(8,128)(2,1)}), bf16[512,8192]{0,1:T(8,128)(2,1)}) %all-gather.4.cloned.1.call-update) | async-done | bytes 8388624 | tf_op jit(solution)/shard_map/all_gather | solution.py:171
  607.8 15.6 %fusion.63 = bf16[1,512,1024]{2,1,0:T(8,128)(2,1)} fusion(bf16[512,8192]{0,1:T(8,128)(2,1)} %all-gather.4.cloned.1.call-done, bf16[8192,1024]{1,0:T(8,128)(2,1)} %get-tuple-element.209), kind=kOutput, calls=%fused_computation.79 | convolution fusion | flops 8590458880 | bytes 26214400 | tf_op jit(solution)/shard_map/dot_general | solution.py:170
  (30 shorter events, 0.3 us)
Async XLA Ops:
  6.5 246.8 %all-gather.6.cloned.1.call-start = ((), (), s32[]{:S(2)}) async-start(), calls=%async_computation.3 | async-start | bytes 9437184 | tf_op jit(solution)/shard_map/all_gather | solution.py:139
  13.7 14.8 %all-to-all-start.1 = ((bf16[8,8,1024]{2,0,1:T(8,128)(2,1)}), bf16[8,8,1024]{2,0,1:T(8,128)(2,1)S(1)}, u32[]{:S(2)}, u32[]{:S(2)}) async-start(bf16[8,8,1024]{2,0,1:T(8,128)(2,1)} %bitcast.31), calls=%async_computation.1 | async-start | bytes 262144 | tf_op jit(solution)/shard_map/all_to_all | solution.py:167
  21.0 12.2 %copy-start.7 = (s32[16]{0:T(128)S(1)}, s32[16]{0:T(128)}, u32[]{:S(2)}) copy-start(s32[16]{0:T(128)} %param.26) | copy-start | bytes 196
  21.0 12.6 %copy-start.3 = (bf16[64,1024]{1,0:T(8,128)(2,1)S(1)}, bf16[64,1024]{1,0:T(8,128)(2,1)}, u32[]{:S(2)}) copy-start(bf16[64,1024]{1,0:T(8,128)(2,1)} %param.20) | copy-start | bytes 393220
  21.0 12.7 %copy-start.6 = (bf16[8192]{0:T(1024)(128)(2,1)S(1)}, bf16[8192]{0:T(1024)(128)(2,1)}, u32[]{:S(2)}) copy-start(bf16[8192]{0:T(1024)(128)(2,1)} %param.18) | copy-start | bytes 49156
  21.0 13.0 %copy-start = (s32[32]{0:T(128)S(1)}, s32[32]{0:T(128)}, u32[]{:S(2)}) copy-start(s32[32]{0:T(128)} %param.27) | copy-start | bytes 388
  28.5 7.6 %copy-start.4 = (bf16[1,64,256]{2,1,0:T(8,128)(2,1)S(1)}, bf16[1,64,256]{2,1,0:T(8,128)(2,1)}, u32[]{:S(2)}) copy-start(bf16[1,64,256]{2,1,0:T(8,128)(2,1)} %param.22) | copy-start | bytes 98308
  28.5 7.6 %copy-start.2 = (s32[1,1024,256]{2,1,0:T(8,128)S(1)}, s32[1,1024,256]{2,1,0:T(8,128)}, u32[]{:S(2)}) copy-start(s32[1,1024,256]{2,1,0:T(8,128)} %param.21) | copy-start | bytes 3145732
  28.5 180.5 %all-to-all-start = ((s32[128,8,1024]{0,2,1:T(8,128)}), s32[128,8,1024]{0,2,1:T(8,128)}, u32[]{:S(2)}, u32[]{:S(2)}) async-start(s32[128,8,1024]{0,2,1:T(8,128)} %bitcast.139), calls=%async_computation | async-start | bytes 8388608 | tf_op jit(solution)/shard_map/all_to_all | solution.py:166
  33.1 6.3 copy-start.5
  33.2 6.4 %copy-start.8 = (s32[496]{0:T(512)S(1)}, s32[496]{0:T(512)}, u32[]{:S(2)}) copy-start(s32[496]{0:T(512)} %param.29) | copy-start | bytes 5956
  33.2 574.6 %all-gather.4.cloned.1.call-start = ((), (), s32[]{:S(2)}) async-start(), calls=%async_computation.2 | async-start | bytes 9437184 | tf_op jit(solution)/shard_map/all_gather | solution.py:171
  253.3 5.8 copy-start.1
  264.8 14.3 %collective-permute-start = (bf16[512,256]{0,1:T(8,128)(2,1)S(1)}, bf16[512,256]{0,1:T(8,128)(2,1)S(1)}, u32[]{:S(2)}, u32[]{:S(2)}) collective-permute-start(bf16[512,256]{0,1:T(8,128)(2,1)S(1)} %pad_maximum_fusion.1), channel_id=1, source_target_pairs={{0,1},{2,3},{4,5},{6,7},{8,9},{10,11},{12,13},{14,15},{16,17},{18,... | collective-permute-start | bytes 786440 | tf_op jit(solution)/shard_map/ppermute | solution.py:12
Sparse Core Ops, SparseCore 0:
  13.8 207.2 all-gather.5
  290.9 316.7 all-gather.3
where the time goes:
time: 632 us; the launch traced here: 630 us
  waiting for transfers between devices  487 us (77%)
  local copies, waits for them, and re-layouts  44 us (7%)
  matrix products  42.8 us (7%)
  other arithmetic  28.7 us (5%)
  between operations  13.7 us (2%)
  starting transfers between devices  13.6 us (2%)
    all_gather x1, waiting for transfers between devices, local(): lax.all_gather(attention_output, 'tp', axis=1, tiled=True)  317 us
    all_to_all x1, waiting for transfers between devices, local(): lax.all_to_all(o_words, 'tp', split_axis=1, concat_axis=0, tiled=True)  169 us
    dot_general x1, local copies, waits for them, and re-layouts, local(): projected = jnp.dot(normed, w_query, preferred_element_type=jnp.float32)  21.3 us
    convert_element_type x2, other arithmetic, unpack_words(): return (values * spread).astype(jnp.bfloat16)  21 us
    dot_general x1, matrix products, local(): jnp.dot(lax.all_gather(attention_output, 'tp', axis=1, tiled=True), w_col...  15.6 us
    unnamed x20, local copies, waits for them, and re-layouts  13.5 us
  transfers between devices with their start and end apart: 5, of which 3 were waited for; matrix products, arithmetic and copies ran while one was open for 11% of the time, Pallas kernels for 0%

commit v1 on v0

--- a/solution.py
+++ b/solution.py
@@ -4,6 +4,12 @@
 from jax.sharding import PartitionSpec as P
 
 HD = 128
+
+
+def gathered_along(x, axis, along):
+    parts = lax.all_gather(x, axis, axis=0, tiled=False)
+    whole = jnp.concatenate(parts, axis=along)
+    return whole
 
 
 def passed_along(block, axis, distance):
@@ -168,9 +174,7 @@
     )
     w_columns = unpack_words(column_words, column_scales)
     summed = jnp.dot(
-        lax.all_gather(attention_output, "tp", axis=1, tiled=True),
-        w_columns,
-        preferred_element_type=jnp.float32,
+        gathered_along(attention_output, "tp", 1), w_columns, preferred_element_type=jnp.float32
     )
     return summed.astype(jnp.bfloat16)[None]
 

time: 632 us -> 577 us (0.913); the launches traced: 630 us -> 568 us
  waiting for transfers between devices: 487 us -> 406 us
  local copies, waits for them, and re-layouts: 44 us -> 63.1 us
    all_to_all x1, waiting for transfers between devices: 169 us -> 50 us  [local(): lax.all_to_all(o_words, 'tp', split_axis=1, concat_axis=0, tiled=True)]
    all_gather x1, waiting for transfers between devices: 0.01 us -> 87.4 us  [local(): whole = lax.all_gather(rows_in[0], 'tp', axis=1, tiled=True)]
    all_gather x1, waiting for transfers between devices: 317 us -> 267 us  [gathered_along(): parts = lax.all_gather(x, axis, axis=0, tiled=False)]
    all_gather x0 -> x1, local copies, waits for them, and re-layouts: none -> 11.4 us  [gathered_along(): parts = lax.all_gather(x, axis, axis=0, tiled=False)]
    shift_right_arithmetic x2 -> x5, local copies, waits for them, and re-layouts: 0.29 us -> 7.57 us  [unpack_words(): jnp.right_shift(words[:, None, :], shifts[None, :, None])]
    convert_element_type x2 -> x3, other arithmetic: 21 us -> 24.6 us  [unpack_words(): return (values * spread).astype(jnp.bfloat16)]
    unnamed x20 -> x24, local copies, waits for them, and re-layouts: 13.5 us -> 13.3 us
  transfers between devices with their start and end apart: 5 -> 5, of which waited for: 3 -> 4; matrix products, arithmetic and copies ran while one was open for 11% -> 14% of each run, Pallas kernels for 0% -> 0%
where the time goes in v1:
time: 577 us; the launch traced here: 568 us
  waiting for transfers between devices  406 us (70%)
  local copies, waits for them, and re-layouts  63.1 us (11%)
  matrix products  42.8 us (7%)
  other arithmetic  32.3 us (6%)
  between operations  13.7 us (2%)
  starting transfers between devices  9.68 us (2%)
    all_gather x1, waiting for transfers between devices, gathered_along(): parts = lax.all_gather(x, axis, axis=0, tiled=False)  267 us
    all_gather x1, waiting for transfers between devices, local(): whole = lax.all_gather(rows_in[0], 'tp', axis=1, tiled=True)  87.4 us
    all_to_all x1, waiting for transfers between devices, local(): lax.all_to_all(o_words, 'tp', split_axis=1, concat_axis=0, tiled=True)  50 us
    convert_element_type x3, other arithmetic, unpack_words(): return (values * spread).astype(jnp.bfloat16)  24.6 us
    dot_general x1, local copies, waits for them, and re-layouts, local(): projected = jnp.dot(normed, w_query, preferred_element_type=jnp.float32)  21.4 us
    dot_general x1, matrix products, local(): jnp.dot(gathered_along(attention_output, 'tp', 1), w_columns, preferred_e...  15.6 us
    unnamed x24, local copies, waits for them, and re-layouts  13.3 us
    dot_general x1, matrix products, local(): projected = jnp.dot(normed, w_query, preferred_element_type=jnp.float32)  12.3 us
  transfers between devices with their start and end apart: 5, of which 4 were waited for; matrix products, arithmetic and copies ran while one was open for 14% of the time, Pallas kernels for 0%

profile of v1, /device:TPU:0, one launch (start us, length us, event | category | flops | bytes accessed | tf_op | source)
XLA Modules:
  0.0 567.8 jit_solution(13126002758650348179)
XLA Ops:
  6.5 7.2 %copy.118 = bf16[1,1024,16,256]{3,2,1,0:T(8,128)(2,1)} copy(bf16[1,1024,16,256]{3,2,1,0:T(8,128)(2,1)} %param.25) | data formatting | bytes 16777216
  13.7 0.0 all-gather.6.cloned.1.call-update
  13.7 0.0 all-gather.4.cloned.1.call-start
  13.8 0.1 copy.63
  13.9 0.1 multiply_reduce_fusion
  14.0 0.1 compare_select_fusion.2
  14.1 0.1 reshape.384
  14.2 1.9 gather_fusion.1
  16.1 0.1 reshape.383
  16.2 0.1 copy.65
  16.4 0.3 shift_right_arithmetic.75
  16.6 11.3 %fusion.48 = bf16[8192,1024]{1,0:T(8,128)(2,1)} fusion(f32[64,1024]{1,0:T(8,128)S(1)} %convert_element_type.109, s32[8192]{0:T(1024)S(1)} %shift_right_arithmetic.75, s32[1024,1024]{1,0:T(8,128)} %param.19), kind=kLoop, calls=%fused_computation.59 | loop fusion | flops 50331648 | bytes 21266432 | tf_op jit(solution)/shard_map/convert_element_type | solution.py:27
  28.0 0.0 copy-start.5
  28.0 21.4 %copy.85 = bf16[1024,8192]{1,0:T(8,128)(2,1)} copy(bf16[1024,8192]{0,1:T(8,128)(2,1)} %bitcast.141) | data formatting | bytes 33554432 | tf_op jit(solution)/shard_map/dot_general | solution.py:154
  49.4 3.4 fusion.57
  52.8 0.1 pad_add_fusion
  52.8 0.1 select_reduce_fusion.1
  52.9 0.1 select_convert_fusion
  53.0 0.1 fusion.73
  53.1 0.5 multiply_cosine_fusion
  53.6 87.4 %all-gather.6.cloned.1.call-done = bf16[1,512,8192]{2,1,0:T(8,128)(2,1)} async-done(((bf16[1,512,1024]{2,1,0:T(8,128)(2,1)}), bf16[1,512,8192]{2,1,0:T(8,128)(2,1)}) %all-gather.6.cloned.1.call-update) | async-done | bytes 8388624 | tf_op jit(solution)/shard_map/all_gather | solution.py:145
  141.1 5.3 fusion.52
  146.3 0.5 copy-done.1
  146.8 5.1 fusion.62
  152.0 0.6 fusion.70
  152.6 1.5 collective-permute-start
  154.1 12.3 %fusion.55 = f32[512,8,128]{0,2,1:T(8,128)S(1)} fusion(bf16[8,128,8192]{2,1,0:T(8,128)(2,1)} %bitcast.143, bf16[1,512,8192]{2,1,0:T(8,128)(2,1)S(1)} %copy-done.1, f32[8192]{0:T(1024)S(1)} %convert_element_type.100, f32[512]{0:T(512)S(1)} %add_rsqrt_fusion), kind=kOutput, calls=%fused_computation.69 | convolution fusion | flops 8606711808 | bytes 27297792 | tf_op jit(solution)/shard_map/dot_general | solution.py:154
  166.4 0.4 subtract_convert_fusion
  166.7 0.1 pad_maximum_fusion
  166.8 10.1 %conditional.1 = (bf16[512,8,128]{2,0,1:T(8,128)(2,1)S(1)}) conditional(s32[]{:T(128)} %convert_element_type.98, (bf16[1,1024,16,256]{3,2,1,0:T(8,128)(2,1)}, s32[32]{0:T(128)S(1)}, bf16[512,256]{0,1:T(8,128)(2,1)S(1)}, s32[512]{0:T(512)S(1)}, bf16[512,8,128]{0,2,1:T(8,128)(2,1)S(1)}, /*index=5*/s32[512,16]{0,1:T(8,128)S(1)}, ...), branch_computations={%region_3.9_spmd, %region_9.13_spmd} | conditional | flops 1087651840 | bytes 90089928 | solution.py:170
  166.9 0.2 fusion.8
  167.1 5.2 fusion.76
  172.3 4.7 fusion.7
  177.0 0.5 copy.74
  177.5 1.3 copy.75
  178.8 0.0 all-gather.4.cloned.1.call-update
  178.8 3.6 all-to-all-start.1
  182.5 5.6 copy.77
  188.1 1.4 all-to-all-done.1
  189.5 4.5 all-to-all-start
  194.1 0.1 shift_right_arithmetic.86
  194.2 50.0 %all-to-all-done = s32[128,8,1024]{0,2,1:T(8,128)} async-done(((s32[128,8,1024]{0,2,1:T(8,128)}), s32[128,8,1024]{0,2,1:T(8,128)}, u32[]{:S(2)}, u32[]{:S(2)}) %all-to-all-start) | async-done | bytes 4194336 | tf_op jit(solution)/shard_map/all_to_all | solution.py:172
  244.2 5.4 copy.78
  249.6 7.2 %shift_right_arithmetic.83 = s32[1024,8,1024]{2,1,0:T(8,128)S(1)} broadcast(s32[1024,1024]{1,0:T(8,128)} %bitcast.142), dimensions={0,2} | broadcast | bytes 37748736 | tf_op jit(solution)/shard_map/shift_right_arithmetic | solution.py:23
  256.8 9.9 %fusion.47 = bf16[64,128,1024]{2,1,0:T(8,128)(2,1)} fusion(f32[64,1024]{1,0:T(8,128)S(1)} %convert_bitcast_fusion, s32[128]{0:T(128)S(1)} %shift_right_arithmetic.86, s32[64,128,1024]{2,1,0:T(8,128)S(1)} %bitcast.140), kind=kLoop, calls=%fused_computation.57 | loop fusion | flops 50331648 | bytes 50594304 | tf_op jit(solution)/shard_map/convert_element_type | solution.py:27
  266.7 267.2 %all-gather.4.cloned.1.call-done = bf16[8,512,1024]{2,1,0:T(8,128)(2,1)} async-done(((bf16[1,512,1024]{2,1,0:T(8,128)(2,1)}), bf16[8,512,1024]{2,1,0:T(8,128)(2,1)}) %all-gather.4.cloned.1.call-update) | async-done | bytes 8388624 | tf_op jit(solution)/shard_map/all_gather | solution.py:10
  533.9 11.4 %copy.76 = bf16[8,512,1024]{1,2,0:T(8,128)(2,1)} copy(bf16[8,512,1024]{2,1,0:T(8,128)(2,1)} %all-gather.4.cloned.1.call-done) | data formatting | bytes 16777216 | tf_op jit(solution)/shard_map/all_gather | solution.py:10
  545.3 15.6 %fusion.64 = bf16[1,512,1024]{2,1,0:T(8,128)(2,1)} fusion(bf16[512,8192]{0,1:T(8,128)(2,1)} %bitcast.146, bf16[8192,1024]{1,0:T(8,128)(2,1)} %bitcast.144), kind=kOutput, calls=%fused_computation.79 | convolution fusion | flops 8590458880 | bytes 26214400 | tf_op jit(solution)/shard_map/dot_general | solution.py:176
  (40 shorter events, 0.3 us)
Async XLA Ops:
  6.5 7.3 %copy-start.9 = (s32[16]{0:T(128)S(1)}, s32[16]{0:T(128)}, u32[]{:S(2)}) copy-start(s32[16]{0:T(128)} %param.26) | copy-start | bytes 196
  6.5 7.7 %copy-start = (s32[32]{0:T(128)S(1)}, s32[32]{0:T(128)}, u32[]{:S(2)}) copy-start(s32[32]{0:T(128)} %param.27) | copy-start | bytes 388
  6.5 134.5 %all-gather.6.cloned.1.call-start = ((), (), s32[]{:S(2)}) async-start(), calls=%async_computation.3 | async-start | bytes 9437184 | tf_op jit(solution)/shard_map/all_gather | solution.py:145
  13.7 2.6 copy-start.6
  13.7 2.6 copy-start.3
  13.7 520.2 %all-gather.4.cloned.1.call-start = ((), (), s32[]{:S(2)}) async-start(), calls=%async_computation.2 | async-start | bytes 9437184 | tf_op jit(solution)/shard_map/all_gather | solution.py:10
  16.3 11.6 %copy-start.7 = (s32[8]{0:T(128)}, s32[8]{0:T(128)S(1)}, u32[]{:S(2)}) copy-start(s32[8]{0:T(128)S(1)} %iota_multiply_fusion.1) | copy-start | bytes 100
  27.9 21.4 %copy-start.4 = (bf16[1,64,256]{2,1,0:T(8,128)(2,1)S(1)}, bf16[1,64,256]{2,1,0:T(8,128)(2,1)}, u32[]{:S(2)}) copy-start(bf16[1,64,256]{2,1,0:T(8,128)(2,1)} %param.22) | copy-start | bytes 98308
  27.9 21.4 %copy-start.2 = (s32[1,1024,256]{2,1,0:T(8,128)S(1)}, s32[1,1024,256]{2,1,0:T(8,128)}, u32[]{:S(2)}) copy-start(s32[1,1024,256]{2,1,0:T(8,128)} %param.21) | copy-start | bytes 3145732
  28.0 24.8 %copy-start.5 = (s32[496,16]{0,1:T(8,128)S(1)}, s32[496,16]{0,1:T(8,128)}, u32[]{:S(2)}) copy-start(s32[496,16]{0,1:T(8,128)} %param.28) | copy-start | bytes 95236
  28.0 25.0 %copy-start.10 = (s32[496]{0:T(512)S(1)}, s32[496]{0:T(512)}, u32[]{:S(2)}) copy-start(s32[496]{0:T(512)} %param.29) | copy-start | bytes 5956
  141.1 5.8 %copy-start.1 = (bf16[1,512,8192]{2,1,0:T(8,128)(2,1)S(1)}, bf16[1,512,8192]{2,1,0:T(8,128)(2,1)}, u32[]{:S(2)}) copy-start(bf16[1,512,8192]{2,1,0:T(8,128)(2,1)} %all-gather.6.cloned.1.call-done) | copy-start | bytes 25165828
  152.6 14.3 %collective-permute-start = (bf16[512,256]{0,1:T(8,128)(2,1)S(1)}, bf16[512,256]{0,1:T(8,128)(2,1)S(1)}, u32[]{:S(2)}, u32[]{:S(2)}) collective-permute-start(bf16[512,256]{0,1:T(8,128)(2,1)S(1)} %pad_maximum_fusion.1), channel_id=1, source_target_pairs={{0,1},{2,3},{4,5},{6,7},{8,9},{10,11},{12,13},{14,15},{16,17},{18,... | collective-permute-start | bytes 786440 | tf_op jit(solution)/shard_map/ppermute | solution.py:18
  178.8 10.7 %all-to-all-start.1 = ((bf16[8,8,1024]{2,0,1:T(8,128)(2,1)}), bf16[8,8,1024]{2,0,1:T(8,128)(2,1)S(1)}, u32[]{:S(2)}, u32[]{:S(2)}) async-start(bf16[8,8,1024]{2,0,1:T(8,128)(2,1)} %bitcast.33), calls=%async_computation.1 | async-start | bytes 262144 | tf_op jit(solution)/shard_map/all_to_all | solution.py:173
  182.5 11.6 %copy-start.8 = (s32[8]{0:T(128)S(1)}, s32[8]{0:T(128)}, u32[]{:S(2)}) copy-start(s32[8]{0:T(128)} %copy-done.7) | copy-start | bytes 100
  189.5 54.7 %all-to-all-start = ((s32[128,8,1024]{0,2,1:T(8,128)}), s32[128,8,1024]{0,2,1:T(8,128)}, u32[]{:S(2)}, u32[]{:S(2)}) async-start(s32[128,8,1024]{0,2,1:T(8,128)} %bitcast.145), calls=%async_computation | async-start | bytes 8388608 | tf_op jit(solution)/shard_map/all_to_all | solution.py:172
Sparse Core Ops, SparseCore 0:
  13.9 127.1 all-gather.5
  179.0 354.9 all-gather.3
